TPU v7x, 32 devices: a whole 2x2x4 slice. The times are simulated.
32 devices in a mesh: gx: 8 (over y, x, core), gy: 4 (over z).
Axes of the slice: x: 2, y: 2, z: 4, core: 2. Of those that a mesh axis runs over, the one named last changes fastest.
Arguments:
- candidate_owner: int32 [256, 512, 1], P(('gx', 'gy')), may hold values from 0 to 31; in each aligned block of 4096 rows (0 to 4095, 4096 to 8191, ..., all dimensions but the last counted through in order) at most 256 rows name the same one
- candidate_row: int32 [256, 512], P(('gx', 'gy')), may hold values from 0 to 78335
- item_table: bfloat16 [2506752, 128], P(('gx', 'gy')), may hold values from -6 to 6
- w_in: bfloat16 [128, 512], replicated, may hold values from -0.5 to 0.5
- w_qkv: bfloat16 [1, 512, 1536], replicated, may hold values from -0.25 to 0.25
- w_out: bfloat16 [1, 512, 512], replicated, may hold values from -0.25 to 0.25
- w_up: bfloat16 [1, 512, 1024], replicated, may hold values from -0.25 to 0.25
- w_down: bfloat16 [1, 1024, 512], replicated, may hold values from -0.1875 to 0.1875
- norm_gains: float32 [1, 2, 512], replicated, may hold values from 0.25 to 1.75
- final_gain: float32 [512], replicated, may hold values from 0.25 to 1.75
- w_score: bfloat16 [512], replicated, may hold values from -0.25 to 0.25
Outputs:
- log_probs: float32 [256, 512], P(('gx', 'gy'))
Inputs may be any that keep to these rules, and one draw needn't show every extreme that they name: `candidate_owner`: among the candidates of one device's 8 slates no shard is named more than 256 times, a bound that some block reaches.
All inputs are finite; a program needn't handle non-finite values.
Results may differ from a plain program's by a relative error of at most 0.0007.
Values may be sent and summed in bfloat16 or wider, within the bound.
A program may use at most 128 MiB of HBM per device.

v0:
```python
import functools
import jax
import jax.numpy as jnp
from jax import lax
from jax.experimental import pallas as pl
from jax.experimental.pallas import tpu as pltpu
from jax.sharding import PartitionSpec as P

HEADS = 8
PICK = 32
CHUNKS = 2
LOG2E = 1.4426950408889634


def layer_norm(values, gain):
    mean = jnp.mean(values, axis=-1, keepdims=True)
    centred = values - mean
    variance = jnp.mean(centred * centred, axis=-1, keepdims=True)
    return centred * lax.rsqrt(variance + 1e-05) * gain


def slate_kernel(chunks, place_ref, *refs):
    returned_refs = refs[:chunks]
    (
        w_in_ref, w_qkv_ref, w_out_ref, w_up_ref, w_down_ref, gains_ref, fgain_ref, score_ref,
        out_ref, rows_ref, emb_ref,
    ) = refs[chunks:]
    f32, bf16 = jnp.float32, jnp.bfloat16
    slate = pl.program_id(0)

    @pl.when(slate == 0)
    def _():
        for chunk, ref in enumerate(returned_refs):
            size = ref.shape[0]
            rows_ref[chunk * size : (chunk + 1) * size, :] = ref[...].astype(f32)

    base = slate * emb_ref.shape[0]

    def pick(block, carry):
        for row in range(PICK):
            index = block * PICK + row
            emb_ref[pl.ds(index, 1), :] = rows_ref[pl.ds(place_ref[base + index], 1), :]
        return carry

    lax.fori_loop(0, emb_ref.shape[0] // PICK, pick, 0)
    model = w_in_ref.shape[1]
    head_dim = model // HEADS
    length = emb_ref.shape[0]
    pack = 128 // head_dim
    resid = jnp.dot(emb_ref[...].astype(bf16), w_in_ref[...], preferred_element_type=f32)
    normed = layer_norm(resid, gains_ref[0:1, :]).astype(bf16)
    query = jnp.dot(normed, w_qkv_ref[:, :model], preferred_element_type=f32)
    query = (query * (LOG2E * head_dim ** (-0.5))).astype(bf16)
    keys = jnp.dot(normed, w_qkv_ref[:, model : 2 * model], preferred_element_type=f32).astype(bf16)
    values = jnp.dot(normed, w_qkv_ref[:, 2 * model :], preferred_element_type=f32).astype(bf16)
    ones = jnp.ones((length, 128), bf16)
    lane = lax.broadcasted_iota(jnp.int32, (length, 128), 1) // head_dim
    mixed = []
    for group in range(HEADS // pack):
        cols = slice(group * 128, (group + 1) * 128)
        q_g, k_g = query[:, cols], keys[:, cols]
        v_g = jnp.concatenate([values[:, cols], ones], axis=1)
        total = None
        for part in range(pack):
            q_h = jnp.where(lane == part, q_g, jnp.zeros_like(q_g))
            scores = lax.dot_general(q_h, k_g, (((1,), (1,)), ((), ())), preferred_element_type=f32)
            top = jnp.max(scores, axis=-1, keepdims=True)
            probs = jnp.exp2(scores - top).astype(bf16)
            both = jnp.dot(probs, v_g, preferred_element_type=f32)
            head = both[:, :128] / both[:, 128:]
            total = head if total is None else jnp.where(lane == part, head, total)
        mixed.append(total.astype(bf16))
    mixed = jnp.concatenate(mixed, axis=1)
    resid = resid + jnp.dot(mixed, w_out_ref[...], preferred_element_type=f32)
    normed = layer_norm(resid, gains_ref[1:2, :]).astype(bf16)
    inner = jax.nn.gelu(jnp.dot(normed, w_up_ref[...], preferred_element_type=f32)).astype(bf16)
    resid = resid + jnp.dot(inner, w_down_ref[...], preferred_element_type=f32)
    terms = layer_norm(resid, fgain_ref[...]) * score_ref[...]
    folded = terms[:, :128]
    for start in range(128, model, 128):
        folded = folded + terms[:, start : start + 128]
    logits = jnp.sum(folded.T, axis=0, keepdims=True)
    shifted = logits - jnp.max(logits, axis=-1, keepdims=True)
    out_ref[0] = shifted - jnp.log(jnp.sum(jnp.exp(shifted), axis=-1, keepdims=True))


def score_slates(returned, position, w_in, w_qkv, w_out, w_up, w_down, norm_gains, final_gain, w_score):
    slates, length = position.shape
    chunks, width = len(returned), returned[0].shape[1]
    weights = (
        w_in,
        w_qkv[0],
        w_out[0],
        w_up[0],
        w_down[0],
        norm_gains[0],
        final_gain[None, :],
        w_score.astype(jnp.float32)[None, :],
    )
    whole = lambda w: pl.BlockSpec(w.shape, lambda s, place: (0, 0))
    out = pl.pallas_call(
        functools.partial(slate_kernel, chunks),
        grid_spec=pltpu.PrefetchScalarGridSpec(
            num_scalar_prefetch=1,
            grid=(slates,),
            in_specs=[whole(w) for w in (*returned, *weights)],
            out_specs=pl.BlockSpec((1, 1, length), lambda s, place: (s, 0, 0)),
            scratch_shapes=[
                pltpu.VMEM((chunks * returned[0].shape[0], width), jnp.float32),
                pltpu.VMEM((length, width), jnp.float32),
            ],
        ),
        out_shape=jax.ShapeDtypeStruct((slates, 1, length), jnp.float32),
        compiler_params=pltpu.CompilerParams(vmem_limit_bytes=60 * 1024 * 1024),
        name="slates",
    )(position.reshape(-1), *returned, *weights)
    return out.reshape(slates, length)


def slots_and_requests(owner, row_index, shards, capacity, length):
    total = owner.shape[0]
    onehot = (owner[:, None] == jnp.arange(shards, dtype=jnp.int32)[None, :]).astype(jnp.bfloat16)
    blocks = onehot.reshape(total // length, length, shards)
    lower = (jnp.arange(length)[:, None] >= jnp.arange(length)[None, :]).astype(jnp.bfloat16)
    within = jnp.einsum("ij,bjn->bin", lower, blocks, preferred_element_type=jnp.float32)
    totals = within[:, -1, :]
    before = jnp.cumsum(totals, axis=0) - totals
    counts = within + before[:, None, :]
    picked = jnp.sum(counts * blocks.astype(jnp.float32), axis=-1)
    slot = (picked.reshape(total) - 1.0).astype(jnp.int32)
    at_slot = (slot[:, None] == jnp.arange(capacity, dtype=jnp.int32)[None, :]).astype(jnp.bfloat16)
    digits = jnp.stack([row_index >> 16, (row_index >> 8) & 255, row_index & 255], axis=1).astype(jnp.bfloat16)
    placed = (onehot[:, None, :] * digits[:, :, None]).reshape(total, 3 * shards)
    found = lax.dot_general(placed, at_slot, (((0,), (0,)), ((), ())), preferred_element_type=jnp.float32)
    found = found.astype(jnp.int32).reshape(3, shards, capacity)
    return slot, (found[0] << 16) + (found[1] << 8) + found[2]


def exchange_kernel(blocks_ref, out_ref, send_sems, recv_sems, own_sem):
    inner = lax.axis_size("gy")
    count = lax.axis_size("gx") * inner
    here = lax.axis_index("gx") * inner + lax.axis_index("gy")
    barrier = pltpu.get_barrier_semaphore()

    def place(step):
        peer = lax.rem(here + step, count)
        return peer, (peer // inner, lax.rem(peer, inner))

    def copy_of(step):
        peer, device = place(step)
        return pltpu.make_async_remote_copy(
            src_ref=blocks_ref.at[peer],
            dst_ref=out_ref.at[here],
            send_sem=send_sems.at[step],
            recv_sem=recv_sems.at[step],
            device_id=device,
            device_id_type=pl.DeviceIdType.MESH,
        )

    @pl.loop(1, count)
    def _(step):
        pl.semaphore_signal(barrier, inc=1, device_id=place(step)[1], device_id_type=pl.DeviceIdType.MESH)

    own = pltpu.make_async_copy(blocks_ref.at[here], out_ref.at[here], own_sem)
    own.start()
    pl.semaphore_wait(barrier, count - 1)

    @pl.loop(1, count)
    def _(step):
        copy_of(step).start()

    @pl.loop(1, count)
    def _(step):
        copy_of(step).wait()

    own.wait()


def exchange(blocks, collective_id, space):
    count = blocks.shape[0]
    return pl.pallas_call(
        exchange_kernel,
        out_shape=jax.ShapeDtypeStruct(blocks.shape, blocks.dtype),
        in_specs=[pl.BlockSpec(memory_space=space)],
        out_specs=pl.BlockSpec(memory_space=space),
        scratch_shapes=[
            pltpu.SemaphoreType.DMA((count,)),
            pltpu.SemaphoreType.DMA((count,)),
            pltpu.SemaphoreType.DMA,
        ],
        compiler_params=pltpu.CompilerParams(
            collective_id=collective_id, has_side_effects=True, vmem_limit_bytes=32 * 1024 * 1024
        ),
        name="exchange",
    )(blocks)


def pick_kernel(asked_ref, table_ref, out_ref, rows_ref, stage_ref):
    step, steps = pl.program_id(0), pl.num_programs(0)
    size = table_ref.shape[0]
    start = pl.multiple_of(step * size, size)
    rows_ref[pl.ds(start, size), :] = table_ref[...].astype(jnp.float32)

    @pl.when(step == steps - 1)
    def _():
        def pick(block, carry):
            for row in range(PICK):
                index = block * PICK + row
                stage_ref[pl.ds(index, 1), :] = rows_ref[pl.ds(asked_ref[index], 1), :]
            return carry

        lax.fori_loop(0, out_ref.shape[0] // PICK, pick, 0)
        out_ref[...] = stage_ref[...].astype(out_ref.dtype)


def pick_rows(item_table, asked):
    rows, width = item_table.shape
    count = asked.shape[0]
    size = next(size for size in range(4608, 0, -16) if rows % size == 0)
    return pl.pallas_call(
        pick_kernel,
        grid_spec=pltpu.PrefetchScalarGridSpec(
            num_scalar_prefetch=1,
            grid=(rows // size,),
            in_specs=[pl.BlockSpec((size, width), lambda s, asked: (s, 0))],
            out_specs=pl.BlockSpec((count, width), lambda s, asked: (0, 0)),
            scratch_shapes=[pltpu.VMEM((rows, width), jnp.float32), pltpu.VMEM((count, width), jnp.float32)],
        ),
        out_shape=jax.ShapeDtypeStruct((count, width), item_table.dtype),
        compiler_params=pltpu.CompilerParams(vmem_limit_bytes=60 * 1024 * 1024),
        name="pick_rows",
    )(asked, item_table)


def per_device(
    candidate_owner,
    candidate_row,
    item_table,
    w_in,
    w_qkv,
    w_out,
    w_up,
    w_down,
    norm_gains,
    final_gain,
    w_score,
):
    slates, length, unused = candidate_owner.shape
    width = item_table.shape[1]
    shards = lax.axis_size(("gx", "gy"))
    capacity = max(2, 2 * slates * length // shards)
    owner = candidate_owner.reshape(slates * length)
    row_index = candidate_row.reshape(slates * length)
    slot, outgoing = slots_and_requests(owner, row_index, shards, capacity, length)
    wanted = exchange(outgoing[:, None, :], 0, pltpu.VMEM).reshape(shards, capacity)
    chunks = CHUNKS if capacity % CHUNKS == 0 else 1
    depth = capacity // chunks
    returned = []
    for chunk in range(chunks):
        asked = wanted[:, chunk * depth : (chunk + 1) * depth].reshape(-1)
        found = pick_rows(item_table, asked).reshape(shards, depth, width)
        back = lax.all_to_all(found, ("gx", "gy"), split_axis=0, concat_axis=0, tiled=True)
        returned.append(back.reshape(shards * depth, width))
    position = (slot // depth) * (shards * depth) + owner * depth + slot % depth
    position = position.reshape(slates, length)
    return score_slates(
        returned, position, w_in, w_qkv, w_out, w_up, w_down, norm_gains, final_gain, w_score
    )


def solution(mesh):
    return jax.shard_map(
        per_device,
        mesh=mesh,
        in_specs=(
            P(("gx", "gy"), None, None),
            P(("gx", "gy"), None),
            P(("gx", "gy"), None),
            P(),
            P(),
            P(),
            P(),
            P(),
            P(),
            P(),
            P(),
        ),
        out_specs=P(("gx", "gy"), None),
        check_vma=False,
    )
```

profile of v0, /device:TPU:0, one launch (start us, length us, event | category | flops | bytes accessed | tf_op | source)
XLA Modules:
  0.0 156.7 jit_solution(10334667758274662063)
XLA Ops:
  0.0 0.7 fusion.17
  0.8 0.7 copy.25
  1.5 0.8 fusion.6
  2.3 0.3 convolution_bitcast_fusion
  2.6 0.2 fusion.20
  2.8 0.2 multiply_reduce_fusion
  3.1 0.1 pad_maximum_fusion
  3.1 0.1 broadcast_multiply_fusion
  3.2 0.9 fusion.2
  4.2 10.6 %exchange.1 = s32[32,1,256]{2,1,0:T(1,128)S(1)} custom-call(s32[32,1,256]{2,1,0:T(1,128)S(1)} %add.49.blocks_ref), custom_call_target="tpu_custom_call" | custom-call | tf_op jit(solution)/shard_map/exchange/pallas_call | solution.py:181
  14.8 0.6 slice_bitcast_fusion
  15.4 19.2 %pick_rows.2 = bf16[4096,128]{1,0:T(8,128)(2,1)} custom-call(s32[4096]{0:T(1024)} %get-tuple-element.6.asked_ref, bf16[78336,128]{1,0:T(8,128)(2,1)} %table_ref.3), custom_call_target="tpu_custom_call" | custom-call | tf_op jit(solution)/shard_map/pick_rows/pallas_call | solution.py:220
  34.6 4.9 %all-to-all-start = ((bf16[32,128,128]{2,1,0:T(8,128)(2,1)}), bf16[32,128,128]{2,1,0:T(8,128)(2,1)S(1)}, u32[]{:S(2)}, u32[]{:S(2)}) async-start(bf16[32,128,128]{2,1,0:T(8,128)(2,1)} %bitcast.53), calls=%async_computation | async-start | bytes 2097152 | tf_op jit(solution)/shard_map/all_to_all | solution.py:262
  39.5 0.0 copy-start.3
  39.5 0.0 copy-start.2
  39.5 19.4 %pick_rows.3 = bf16[4096,128]{1,0:T(8,128)(2,1)} custom-call(s32[4096]{0:T(1024)} %get-tuple-element.5.asked_ref, bf16[78336,128]{1,0:T(8,128)(2,1)} %table_ref.3), custom_call_target="tpu_custom_call" | custom-call | tf_op jit(solution)/shard_map/pick_rows/pallas_call | solution.py:220
  58.9 5.5 %all-to-all-done = bf16[32,128,128]{2,1,0:T(8,128)(2,1)S(1)} async-done(((bf16[32,128,128]{2,1,0:T(8,128)(2,1)}), bf16[32,128,128]{2,1,0:T(8,128)(2,1)S(1)}, u32[]{:S(2)}, u32[]{:S(2)}) %all-to-all-start) | async-done | bytes 1048608 | tf_op jit(solution)/shard_map/all_to_all | solution.py:262
  64.4 0.0 copy-start
  64.4 4.6 %all-to-all-start.1 = ((bf16[32,128,128]{2,1,0:T(8,128)(2,1)}), bf16[32,128,128]{2,1,0:T(8,128)(2,1)S(1)}, u32[]{:S(2)}, u32[]{:S(2)}) async-start(bf16[32,128,128]{2,1,0:T(8,128)(2,1)} %bitcast.51), calls=%async_computation.1 | async-start | bytes 2097152 | tf_op jit(solution)/shard_map/all_to_all | solution.py:262
  69.0 0.0 copy-done.3
  69.0 0.6 broadcast_in_dim.9
  69.6 0.0 copy-done.2
  69.6 0.6 fusion.12.place_ref
  70.2 23.7 %all-to-all-done.1 = bf16[32,128,128]{2,1,0:T(8,128)(2,1)S(1)} async-done(((bf16[32,128,128]{2,1,0:T(8,128)(2,1)}), bf16[32,128,128]{2,1,0:T(8,128)(2,1)S(1)}, u32[]{:S(2)}, u32[]{:S(2)}) %all-to-all-start.1) | async-done | bytes 1048608 | tf_op jit(solution)/shard_map/all_to_all | solution.py:262
  93.9 0.0 copy-start.1
  93.9 0.0 copy-done
  93.9 1.0 copy-done.1
  94.9 60.4 %slates.1 = f32[8,1,512]{2,1,0:T(1,128)} custom-call(s32[4096]{0:T(1024)} %fusion.12.place_ref, bf16[4096,128]{1,0:T(8,128)(2,1)} %bitcast.50, bf16[4096,128]{1,0:T(8,128)(2,1)} %bitcast.52, bf16[128,512]{1,0:T(8,128)(2,1)} %refs_2_.1, bf16[512,1536]{1,0:T(8,128)(2,1)} %bitcast.54, bf16[512,512]{1,0:T(8,128)(2,1)} %bitcast.58, bf16[512,1024]{1,0:T(8,128)(2,1)} %bitcast.55, ...), custom_call_target="tpu_custom_call" | custom-call | tf_op jit(solution)/shard_map/slates/pallas_call | solution.py:101
  155.3 1.3 copy.24
  (8 shorter events, 0.1 us)
Async XLA Ops:
  34.6 29.8 %all-to-all-start = ((bf16[32,128,128]{2,1,0:T(8,128)(2,1)}), bf16[32,128,128]{2,1,0:T(8,128)(2,1)S(1)}, u32[]{:S(2)}, u32[]{:S(2)}) async-start(bf16[32,128,128]{2,1,0:T(8,128)(2,1)} %bitcast.53), calls=%async_computation | async-start | bytes 2097152 | tf_op jit(solution)/shard_map/all_to_all | solution.py:262
  39.5 29.5 %copy-start.3 = (bf16[512]{0:T(512)(128)(2,1)S(1)}, bf16[512]{0:T(512)(128)(2,1)}, u32[]{:S(2)}) copy-start(bf16[512]{0:T(512)(128)(2,1)} %param.21) | copy-start | bytes 3076
  39.5 30.1 %copy-start.2 = (s32[8,512,1]{1,2,0:T(1,128)S(1)}, s32[8,512,1]{1,2,0:T(1,128)}, u32[]{:S(2)}) copy-start(s32[8,512,1]{1,2,0:T(1,128)} %param.11) | copy-start | bytes 49156
  64.4 29.5 %copy-start = (bf16[32,128,128]{2,1,0:T(8,128)(2,1)}, bf16[32,128,128]{2,1,0:T(8,128)(2,1)S(1)}, u32[]{:S(2)}) copy-start(bf16[32,128,128]{2,1,0:T(8,128)(2,1)S(1)} %all-to-all-done) | copy-start | bytes 3145732
  64.4 29.5 %all-to-all-start.1 = ((bf16[32,128,128]{2,1,0:T(8,128)(2,1)}), bf16[32,128,128]{2,1,0:T(8,128)(2,1)S(1)}, u32[]{:S(2)}, u32[]{:S(2)}) async-start(bf16[32,128,128]{2,1,0:T(8,128)(2,1)} %bitcast.51), calls=%async_computation.1 | async-start | bytes 2097152 | tf_op jit(solution)/shard_map/all_to_all | solution.py:262
  93.9 1.0 copy-start.1
where the time goes:
time: 159 us; the launch traced here: 157 us
  Pallas kernels  110 us (69%)
  waiting for transfers between devices  29.2 us (18%)
  starting transfers between devices  9.42 us (6%)
  local copies, waits for them, and re-layouts  3.77 us (2%)
  other arithmetic  3.26 us (2%)
    pallas_call x1, Pallas kernels, score_slates(): pl.pallas_call(functools.partial(slate_kernel, chunks), grid_spec=pltpu.P...  60.4 us
    pallas_call x2, Pallas kernels, pick_rows(): pl.pallas_call(pick_kernel, grid_spec=pltpu.PrefetchScalarGridSpec(num_sc...  38.6 us
    all_to_all x2, waiting for transfers between devices, per_device(): lax.all_to_all(found, ('gx', 'gy'), split_axis=0, concat_axis=0, tiled=True)  29.2 us
    pallas_call x1, Pallas kernels, exchange(): pl.pallas_call(exchange_kernel, out_shape=jax.ShapeDtypeStruct(blocks.sha...  10.6 us
    all_to_all x2, starting transfers between devices, per_device(): lax.all_to_all(found, ('gx', 'gy'), split_axis=0, concat_axis=0, tiled=True)  9.42 us
  transfers between devices with their start and end apart: 2, of which 2 were waited for; matrix products, arithmetic and copies ran while one was open for 1% of the time, Pallas kernels for 12%

commit v1 on v0

v1 whole, which is shorter than its diff:
```python
import functools
import math
import jax
import jax.numpy as jnp
from jax import lax
from jax.experimental import pallas as pl
from jax.experimental.pallas import tpu as pltpu
from jax.sharding import PartitionSpec as P

HEADS = 8
PICK = 32
BUFFERS = 3
EARLY = 5
LOG2E = 1.4426950408889634
LIMIT = 2.0**60
f32, bf16, i32 = jnp.float32, jnp.bfloat16, jnp.int32
MESH = pl.DeviceIdType.MESH


def chunk_ends(capacity):
    return sorted({-(-capacity * part // 128) * 16 for part in (2, 4, 5, 6, 7, 8)})


def ready_chunks(capacity, slates):
    ends, ready = chunk_ends(capacity), []
    for slate in range(slates):
        part = (slate + 1) / slates
        need = min(capacity, capacity * part + 4 * math.sqrt(capacity * part * (1 - part) * (1 - 1 / 16)))
        ready.append(next(chunk for chunk, end in enumerate(ends) if end >= need))
    return ready


def block_size(rows):
    return next(size for size in range(4608, 0, -16) if rows % size == 0)


def norm_cols(values, gain):
    scale = 1.0 / values.shape[0]
    mean = jnp.sum(values, axis=0, keepdims=True) * scale
    centred = values - mean
    variance = jnp.sum(centred * centred, axis=0, keepdims=True) * scale
    return centred * lax.rsqrt(variance + 1e-05) * gain


def score_slate(emb, weights, gain_of, scratch, exact):
    w_in, w_qkv, w_out, w_up, w_down = weights
    resid_ref, query_ref, keys_ref, value_ref, mixed_ref = scratch
    model, length = w_in.shape[0], emb.shape[0]
    head_dim = model // HEADS
    pack = 128 // head_dim
    resid = lax.dot_general(w_in[...], emb, (((1,), (1,)), ((), ())), preferred_element_type=f32)
    resid_ref[...] = resid
    normed = norm_cols(resid, gain_of(0)).astype(bf16)
    keys_ref[...] = jnp.dot(w_qkv[model : 2 * model], normed, preferred_element_type=f32).astype(bf16).T
    query = jnp.dot(w_qkv[:model], normed, preferred_element_type=f32)
    query_ref[...] = (query * (LOG2E * head_dim ** (-0.5))).astype(bf16)
    value_ref[...] = jnp.dot(w_qkv[2 * model :], normed, preferred_element_type=f32).astype(bf16)
    zeros = jnp.zeros((head_dim, length), bf16)
    ones = jnp.ones((16, length), bf16)

    def scores_of(head):
        group, part = head // pack, head % pack
        query = query_ref[head * head_dim : (head + 1) * head_dim, :]
        query = jnp.concatenate([query if p == part else zeros for p in range(pack)], axis=0)
        return jnp.dot(keys_ref[:, group * 128 : (group + 1) * 128], query, preferred_element_type=f32)

    low = high = None
    ahead = scores_of(0)
    for head in range(HEADS):
        rows = slice(head * head_dim, (head + 1) * head_dim)
        scores = ahead
        if head + 1 < HEADS:
            ahead = scores_of(head + 1)
        if exact:
            scores = scores - jnp.max(scores, axis=0, keepdims=True)
        probs = jnp.exp2(scores).astype(bf16)
        stacked = jnp.concatenate([value_ref[rows, :], ones], axis=0)
        both = jnp.dot(stacked, probs, preferred_element_type=f32)
        total = both[head_dim : head_dim + 1]
        low = total if low is None else jnp.minimum(low, total)
        high = total if high is None else jnp.maximum(high, total)
        mixed_ref[rows, :] = (both[:head_dim] * (1.0 / total)).astype(bf16)
    resid = resid_ref[...] + jnp.dot(w_out[...], mixed_ref[...], preferred_element_type=f32)
    resid_ref[...] = resid
    normed = norm_cols(resid, gain_of(1)).astype(bf16)
    inner = jnp.dot(w_up[...], normed, preferred_element_type=f32)
    half = 0.5 * inner
    inner = half + half * jnp.tanh(inner * (0.7978845608028654 + 0.035677408136300125 * (inner * inner)))
    resid = resid_ref[...] + jnp.dot(w_down[...], inner.astype(bf16), preferred_element_type=f32)
    logits = jnp.sum(norm_cols(resid, gain_of(2)) * gain_of(3), axis=0, keepdims=True)
    shifted = logits - jnp.max(logits, axis=-1, keepdims=True)
    result = shifted - jnp.log(jnp.sum(jnp.exp(shifted), axis=-1, keepdims=True))
    return result, low, high


def score_scratch(model, length):
    return [
        pltpu.VMEM((model, length), f32),
        pltpu.VMEM((model, length), bf16),
        pltpu.VMEM((length, model), bf16),
        pltpu.VMEM((model, length), bf16),
        pltpu.VMEM((model, length), bf16),
    ]


def turn_weights(raw, turned):
    for source, target in zip(raw, turned):
        rows, cols = source.shape
        for row in range(0, rows, 512):
            for col in range(0, cols, 512):
                r, c = slice(row, min(rows, row + 512)), slice(col, min(cols, col + 512))
                target[c, r] = source[r, c].T


def spread_gains(gain_refs, target, base):
    norm_ref, final_ref, score_ref = gain_refs
    model = norm_ref.shape[1]
    gains = [norm_ref[...], final_ref[...], score_ref[...].astype(f32), jnp.zeros((4, model), f32)]
    columns = jnp.concatenate(gains, axis=0).T
    for row in range(4):
        target[base + row * model : base + (row + 1) * model, :] = jnp.broadcast_to(
            columns[:, row : row + 1], (model, 128)
        )


def widen(gains_ref, base, row, model, length):
    gain = gains_ref[base + row * model : base + (row + 1) * model, :]
    return jnp.concatenate([gain] * (length // 128), axis=1)


def route(owner_ref, row_ref, asks_ref, place_ref, capacity, shards, rows, bounds):
    slates, length = owner_ref.shape
    ends = chunk_ends(capacity)
    shard = lax.broadcasted_iota(i32, (shards, length), 0)
    slots = lax.broadcasted_iota(i32, (capacity, length), 0)
    upper = lax.broadcasted_iota(i32, (length, length), 0) <= lax.broadcasted_iota(i32, (length, length), 1)
    upper = upper.astype(f32).astype(bf16)
    hits = [(owner_ref[b : b + 1, :] == shard).astype(f32) for b in range(slates)]
    within = jnp.dot(jnp.concatenate(hits, axis=0).astype(bf16), upper, preferred_element_type=f32)
    before = jnp.zeros((shards, 1), f32)
    found, late = None, None
    for b in range(slates):
        counts = within[b * shards : (b + 1) * shards]
        slot = jnp.sum(hits[b] * (counts + before), axis=0, keepdims=True).astype(i32) - 1
        before = before + counts[:, length - 1 : length]
        owner, index = owner_ref[b : b + 1, :], row_ref[b : b + 1, :]
        place = owner * ends[0] + slot
        for start, end in zip(ends[:-1], ends[1:]):
            here = shards * start + owner * (end - start) + (slot - start)
            place = jnp.where(slot >= start, here, place)
        place_ref[b : b + 1, :] = jnp.clip(place, 0, shards * capacity - 1)
        over = (slot >= bounds[b]).astype(i32)
        late = over if late is None else jnp.maximum(late, over)
        at_slot = (slot == slots).astype(f32).astype(bf16)
        digits = (index >> 16, (index >> 8) & 255, index & 255)
        placed = jnp.concatenate([hits[b] * digit.astype(f32) for digit in digits], axis=0).astype(bf16)
        part = lax.dot_general(placed, at_slot, (((1,), (1,)), ((), ())), preferred_element_type=f32)
        found = part if found is None else found + part
    found = found.astype(i32)
    asks = (found[:shards] << 16) + (found[shards : 2 * shards] << 8) + found[2 * shards :]
    asks = jnp.clip(asks, 0, rows - 1)
    for peer in range(shards):
        asks_ref[peer] = asks[peer : peer + 1, :]
    return late


def rank_kernel(capacity, owner_ref, row_ref, norm_ref, final_ref, score_ref, table_ref, *refs):
    chunks = len(chunk_ends(capacity))
    raw_hbm, refs = refs[:5], refs[5:]
    out_ref, flag_ref, place_ref = refs[:3]
    kept_refs, refs = refs[3 : 3 + chunks], refs[3 + chunks :]
    rows_ref, stream_ref, asks_ref, wanted_ref, wanted_smem, place_smem, stage_ref, emb_ref, worst_ref = refs[:9]
    send_refs, refs = refs[9 : 9 + chunks], refs[9 + chunks :]
    recv_refs, refs = refs[:chunks], refs[chunks:]
    raw, turned, refs = refs[:5], refs[5:10], refs[10:]
    scratch, refs = refs[:5], refs[5:]
    (
        stream_sems, raw_sems, ask_send_sem, ask_recv_sem, smem_sems,
        send_sems, recv_sems, keep_sems,
    ) = refs
    inner = lax.axis_size("gy")
    count = lax.axis_size("gx") * inner
    here = lax.axis_index("gx") * inner + lax.axis_index("gy")
    slates, length = owner_ref.shape
    model = norm_ref.shape[1]
    ends = chunk_ends(capacity)
    starts = [0] + ends[:-1]
    ready = ready_chunks(capacity, slates)
    barrier = pltpu.get_barrier_semaphore()

    def peer_of(step):
        peer = lax.rem(here + step, count)
        return peer, (peer // inner, lax.rem(peer, inner))

    @pl.loop(1, count)
    def _(step):
        pl.semaphore_signal(barrier, inc=1, device_id=peer_of(step)[1], device_id_type=MESH)

    size = stream_ref.shape[1]
    blocks = table_ref.shape[0] // size

    def stream(block):
        slot = lax.rem(block, BUFFERS)
        return pltpu.make_async_copy(
            table_ref.at[pl.ds(pl.multiple_of(block * size, size), size)], stream_ref.at[slot], stream_sems.at[slot]
        )

    for block in range(min(BUFFERS, blocks)):
        stream(block).start()
    copies = [pltpu.make_async_copy(s, t, raw_sems.at[n]) for n, (s, t) in enumerate(zip(raw_hbm, raw))]
    for copy in copies:
        copy.start()

    def load(block):
        stream(block).wait()
        start = pl.multiple_of(block * size, size)
        rows_ref[pl.ds(start, size), :] = stream_ref[lax.rem(block, BUFFERS)].astype(f32)

        @pl.when(block + BUFFERS < blocks)
        def _():
            stream(block + BUFFERS).start()

    late = route(
        owner_ref, row_ref, asks_ref, place_ref, capacity, count, table_ref.shape[0], [ends[chunk] for chunk in ready]
    )
    place_copy = pltpu.make_async_copy(place_ref, place_smem, smem_sems.at[0])
    place_copy.start()

    early = min(EARLY, blocks)

    @pl.loop(0, early)
    def _(block):
        load(block)

    def ask(step):
        peer, device = peer_of(step)
        return pltpu.make_async_remote_copy(
            src_ref=asks_ref.at[peer],
            dst_ref=wanted_ref.at[here],
            send_sem=ask_send_sem,
            recv_sem=ask_recv_sem,
            device_id=device,
            device_id_type=MESH,
        )

    pl.semaphore_wait(barrier, count - 1)

    @pl.loop(1, count)
    def _(step):
        ask(step).start()

    wanted_ref[here] = asks_ref[here]

    @pl.loop(early, blocks)
    def _(block):
        load(block)

    others = pl.ds(0, count - 1)
    pltpu.make_async_copy(asks_ref.at[others], asks_ref.at[others], ask_send_sem).wait()
    pltpu.make_async_copy(wanted_ref.at[others], wanted_ref.at[others], ask_recv_sem).wait()
    wanted_copy = pltpu.make_async_copy(wanted_ref, wanted_smem, smem_sems.at[1])
    wanted_copy.start()
    wanted_copy.wait()

    def give(chunk, step):
        peer, device = peer_of(step)
        return pltpu.make_async_remote_copy(
            src_ref=send_refs[chunk].at[peer],
            dst_ref=recv_refs[chunk].at[here],
            send_sem=send_sems.at[chunk],
            recv_sem=recv_sems.at[chunk],
            device_id=device,
            device_id_type=MESH,
        )

    def pick(chunk, step):
        peer = peer_of(step)[0]
        depth = ends[chunk] - starts[chunk]
        for row in range(depth):
            index = wanted_smem[peer, 0, starts[chunk] + row]
            stage_ref[row : row + 1, :] = rows_ref[pl.ds(index, 1), :]
        send_refs[chunk][peer] = stage_ref[:depth, :].astype(bf16)

    for chunk in range(chunks):

        @pl.loop(1, count)
        def _(step):
            pick(chunk, step)
            give(chunk, step).start()

        pick(chunk, 0)

    place_copy.wait()
    for copy in copies:
        copy.wait()
    turn_weights(raw, turned)
    gains_base = count * capacity
    spread_gains((norm_ref, final_ref, score_ref), rows_ref, gains_base)

    def keep(chunk):
        return pltpu.make_async_copy(recv_refs[chunk], kept_refs[chunk], keep_sems.at[chunk])

    def take(chunk):
        depth, base = ends[chunk] - starts[chunk], count * starts[chunk]
        landed = recv_refs[chunk]
        pltpu.make_async_copy(landed.at[others], landed.at[others], recv_sems.at[chunk]).wait()
        landed[here] = send_refs[chunk][here]
        keep(chunk).start()

        @pl.loop(0, count)
        def _(peer):
            start = pl.multiple_of(base + peer * depth, 16)
            rows_ref[pl.ds(start, depth), :] = landed[peer].astype(f32)

    @pl.loop(0, slates)
    def _(slate):
        for chunk in range(chunks):
            first = next(s for s in range(slates) if ready[s] >= chunk)

            @pl.when(slate == first)
            def _():
                take(chunk)

        @pl.loop(0, length // PICK)
        def _(block):
            for row in range(PICK):
                index = block * PICK + row
                emb_ref[pl.ds(index, 1), :] = rows_ref[pl.ds(place_smem[slate, index], 1), :]

        gain_of = lambda row: widen(rows_ref, gains_base, row, model, length)
        result, low, high = score_slate(emb_ref[...].astype(bf16), turned, gain_of, scratch, False)
        out_ref[slate] = result
        bad = jnp.where((low > 1.0 / LIMIT) & (high < LIMIT), 0, 1)
        worst_ref[...] = jnp.maximum(jnp.where(slate == 0, late, worst_ref[...]), bad)

    flag_ref[...] = jnp.broadcast_to(jnp.max(worst_ref[...], axis=1, keepdims=True), flag_ref.shape)
    for chunk in range(chunks):
        sent = send_refs[chunk].at[others]
        pltpu.make_async_copy(sent, sent, send_sems.at[chunk]).wait()
        keep(chunk).wait()


def rank(owner, row_index, gains, table, weights, capacity, shards):
    slates, length = owner.shape
    rows, width = table.shape
    model = gains[0].shape[1]
    ends = chunk_ends(capacity)
    depths = [end - start for start, end in zip([0] + ends[:-1], ends)]
    chunks = len(depths)
    vmem, hbm = pl.BlockSpec(memory_space=pltpu.VMEM), pl.BlockSpec(memory_space=pltpu.HBM)
    size = block_size(rows)
    blocks = [(shards, depth, width) for depth in depths]
    tall = max(rows, shards * capacity + 4 * model)
    return pl.pallas_call(
        functools.partial(rank_kernel, capacity),
        out_shape=[
            jax.ShapeDtypeStruct((slates, 1, length), f32),
            jax.ShapeDtypeStruct((1, 128), i32),
            jax.ShapeDtypeStruct((slates, length), i32),
            *[jax.ShapeDtypeStruct(block, bf16) for block in blocks],
        ],
        in_specs=[vmem, vmem, *[vmem] * 3, hbm, *[hbm] * 5],
        out_specs=[vmem, vmem, vmem, *[hbm] * chunks],
        scratch_shapes=[
            pltpu.VMEM((tall, width), f32),
            pltpu.VMEM((BUFFERS, size, width), bf16),
            pltpu.VMEM((shards, 1, capacity), i32),
            pltpu.VMEM((shards, 1, capacity), i32),
            pltpu.SMEM((shards, 1, capacity), i32),
            pltpu.SMEM((slates, length), i32),
            pltpu.VMEM((max(depths), width), f32),
            pltpu.VMEM((length, width), f32),
            pltpu.VMEM((1, length), i32),
            *[pltpu.VMEM(block, bf16) for block in blocks],
            *[pltpu.VMEM(block, bf16) for block in blocks],
            *[pltpu.VMEM(w.shape, bf16) for w in weights],
            *[pltpu.VMEM(w.shape[::-1], bf16) for w in weights],
            *score_scratch(model, length),
            pltpu.SemaphoreType.DMA((BUFFERS,)),
            pltpu.SemaphoreType.DMA((5,)),
            pltpu.SemaphoreType.DMA,
            pltpu.SemaphoreType.DMA,
            pltpu.SemaphoreType.DMA((2,)),
            pltpu.SemaphoreType.DMA((chunks,)),
            pltpu.SemaphoreType.DMA((chunks,)),
            pltpu.SemaphoreType.DMA((chunks,)),
        ],
        compiler_params=pltpu.CompilerParams(
            collective_id=0, has_side_effects=True, vmem_limit_bytes=67043328
        ),
        name="rank",
    )(owner, row_index, *gains, table, *weights)


def finish_kernel(flag_ref, ranked_ref, place_hbm, norm_hbm, final_hbm, score_hbm, *refs):
    raw_hbm, refs = refs[:5], refs[5:]
    chunks = len(refs) - 24
    kept_refs, out_ref, refs = refs[:chunks], refs[chunks], refs[chunks + 1 :]
    rows_ref, landed_ref, emb_ref, place_ref = refs[:4]
    gain_refs, raw, turned, scratch, sem = refs[4:7], refs[7:12], refs[12:17], refs[17:22], refs[22]
    slates, length = out_ref.shape
    model = norm_hbm.shape[1]
    redo = flag_ref[0, 0] > 0

    def fetch(source, target):
        copy = pltpu.make_async_copy(source, target, sem)
        copy.start()
        copy.wait()

    @pl.when(jnp.logical_not(redo))
    def _():
        for slate in range(slates):
            out_ref[slate : slate + 1, :] = ranked_ref[slate]

    @pl.when(redo)
    def _():
        fetch(place_hbm, place_ref)
        for source, target in zip((norm_hbm, final_hbm, score_hbm, *raw_hbm), (*gain_refs, *raw)):
            fetch(source, target)
        turn_weights(raw, turned)
        base = 0
        for kept in kept_refs:
            shards, depth, width = kept.shape
            fetch(kept, landed_ref.at[:, pl.ds(0, depth), :])

            @pl.loop(0, shards)
            def _(peer):
                start = pl.multiple_of(base + peer * depth, 16)
                rows_ref[pl.ds(start, depth), :] = landed_ref[peer, pl.ds(0, depth), :].astype(f32)

            base += shards * depth
        spread_gains(gain_refs, rows_ref, base)
        gain_of = lambda row: widen(rows_ref, base, row, model, length)

        @pl.loop(0, slates)
        def _(slate):
            @pl.loop(0, length // PICK)
            def _(block):
                for row in range(PICK):
                    index = block * PICK + row
                    emb_ref[pl.ds(index, 1), :] = rows_ref[pl.ds(place_ref[slate, index], 1), :]

            result, low, high = score_slate(emb_ref[...].astype(bf16), turned, gain_of, scratch, True)
            out_ref[pl.ds(slate, 1), :] = result


def finish(flag, place, ranked, gains, weights, kept):
    slates, unused, length = ranked.shape
    model = gains[0].shape[1]
    shards, unused, width = kept[0].shape
    deepest = max(block.shape[1] for block in kept)
    capacity = sum(block.shape[1] for block in kept)
    vmem, hbm, smem = [pl.BlockSpec(memory_space=m) for m in (pltpu.VMEM, pltpu.HBM, pltpu.SMEM)]
    return pl.pallas_call(
        finish_kernel,
        out_shape=jax.ShapeDtypeStruct((slates, length), f32),
        in_specs=[smem, vmem, *[hbm] * (9 + len(kept))],
        out_specs=vmem,
        scratch_shapes=[
            pltpu.VMEM((shards * capacity + 4 * model, width), f32),
            pltpu.VMEM((shards, deepest, width), bf16),
            pltpu.VMEM((length, width), f32),
            pltpu.SMEM((slates, length), i32),
            *[pltpu.VMEM(gain.shape, gain.dtype) for gain in gains],
            *[pltpu.VMEM(w.shape, bf16) for w in weights],
            *[pltpu.VMEM(w.shape[::-1], bf16) for w in weights],
            *score_scratch(model, length),
            pltpu.SemaphoreType.DMA,
        ],
        compiler_params=pltpu.CompilerParams(vmem_limit_bytes=60 * 1024 * 1024),
        name="finish",
    )(flag, ranked, place, *gains, *weights, *kept)


def per_device(
    candidate_owner,
    candidate_row,
    item_table,
    w_in,
    w_qkv,
    w_out,
    w_up,
    w_down,
    norm_gains,
    final_gain,
    w_score,
):
    slates, length, unused = candidate_owner.shape
    shards = lax.axis_size(("gx", "gy"))
    capacity = max(16, 2 * slates * length // shards)
    owner = candidate_owner.reshape(slates, length)
    gains = (norm_gains[0], final_gain[None, :], w_score[None, :])
    weights = (w_in, w_qkv[0], w_out[0], w_up[0], w_down[0])
    ranked, flag, place, *kept = rank(owner, candidate_row, gains, item_table, weights, capacity, shards)
    return finish(flag, place, ranked, gains, weights, kept)


def solution(mesh):
    return jax.shard_map(
        per_device,
        mesh=mesh,
        in_specs=(
            P(("gx", "gy"), None, None),
            P(("gx", "gy"), None),
            P(("gx", "gy"), None),
            P(),
            P(),
            P(),
            P(),
            P(),
            P(),
            P(),
            P(),
        ),
        out_specs=P(("gx", "gy"), None),
        check_vma=False,
    )
```

time: 159 us -> 108 us (0.68); the launches traced: 157 us -> 107 us
  waiting for transfers between devices: 29.2 us -> 0 us
  starting transfers between devices: 9.42 us -> 0 us
  Pallas kernels: 110 us -> 105 us
  other arithmetic: 3.26 us -> 0 us
    all_to_all x2 -> x0, waiting for transfers between devices: 29.2 us -> none  [per_device(): lax.all_to_all(found, ('gx', 'gy'), split_axis=0, concat_axis=0, tiled=True)]
    all_to_all x2 -> x0, starting transfers between devices: 9.42 us -> none  [per_device(): lax.all_to_all(found, ('gx', 'gy'), split_axis=0, concat_axis=0, tiled=True)]
    pallas_call x4 -> x2, Pallas kernels: 110 us -> 105 us  [the longest x1 103 us: rank(): pl.pallas_call(functools.partial(rank_kernel, capacity), out_shape=[jax.S...]
    unnamed x15 -> x1, local copies, waits for them, and re-layouts: 3.13 us -> 1.32 us
  transfers between devices with their start and end apart: 2 -> 0, of which waited for: 2 -> 0; matrix products, arithmetic and copies ran while one was open for 1% -> 0% of each run, Pallas kernels for 12% -> 0%
where the time goes in v1:
time: 108 us; the launch traced here: 107 us
  Pallas kernels  105 us (97%)
  local copies, waits for them, and re-layouts  2.59 us (2%)
    pallas_call x1, Pallas kernels, rank(): pl.pallas_call(functools.partial(rank_kernel, capacity), out_shape=[jax.S...  103 us

profile of v1, /device:TPU:0, one launch (start us, length us, event | category | flops | bytes accessed | tf_op | source)
XLA Modules:
  0.0 107.4 jit_solution(16475497307204120129)
XLA Ops:
  0.0 1.3 %broadcast_in_dim.7.score_ref.score_hbm = bf16[1,512]{1,0:T(2,128)(2,1)} reshape(bf16[512]{0:T(512)(128)(2,1)} %param.21) | data formatting | bytes 2048 | tf_op jit(solution)/shard_map/broadcast_in_dim | solution.py:492
  1.3 1.3 %copy.14 = s32[8,512,1]{1,0,2:T(8,128)} copy(s32[8,512,1]{1,2,0:T(1,128)} %param.11) | data formatting | bytes 32768
  2.6 103.1 %rank.1 = (f32[8,1,512]{2,1,0:T(1,128)}, s32[1,128]{1,0:T(1,128)}, s32[8,512]{1,0:T(8,128)}, bf16[32,64,128]{2,1,0:T(8,128)(2,1)}, bf16[32,64,128]{2,1,0:T(8,128...) custom-call(s32[8,512]{1,0:T(8,128)} %bitcast.17, ...), custom_call_target="tpu_custom_call" | custom-call | tf_op jit(solution)/shard_map/rank/pallas_call | solution.py:354
  105.7 1.5 %finish.1 = f32[8,512]{1,0:T(8,128)} custom-call(s32[1,128]{1,0:T(1,128)} %get-tuple-element.14.flag_ref, f32[8,1,512]{2,1,0:T(1,128)} %get-tuple-element.15.ranked_ref, s32[8,512]{1,0:T(8,128)} %get-tuple-element.16.place_hbm, f32[2,512]{1,0:T(2,128)} %bitcast.19, f32[1,512]{1,0:T(1,128)} %bitcast.21, bf16[1,512]{1,0:T(2,128)(2,1)} %broadcast_in_dim.7.score_ref.score_hbm, ...), custom_call_target="tpu_custom_call" | custom-call | tf_op jit(solution)/shard_map/finish/pallas_call | solution.py:454

commit v2 on v1

--- a/solution.py
+++ b/solution.py
@@ -8,7 +8,10 @@
 from jax.sharding import PartitionSpec as P
 
 HEADS = 8
-PICK = 32
+PICK = 64
+AHEAD = 2
+STRIP = 256
+PARTS = 4
 BUFFERS = 3
 EARLY = 5
 LOG2E = 1.4426950408889634
@@ -34,27 +37,35 @@
     return next(size for size in range(4608, 0, -16) if rows % size == 0)
 
 
-def norm_cols(values, gain):
-    scale = 1.0 / values.shape[0]
-    mean = jnp.sum(values, axis=0, keepdims=True) * scale
-    centred = values - mean
+def norm_parts(ref, cols):
+    scale = 1.0 / ref.shape[0]
+    mean = jnp.sum(ref[:, cols], axis=0, keepdims=True) * scale
+    centred = ref[:, cols] - mean
     variance = jnp.sum(centred * centred, axis=0, keepdims=True) * scale
-    return centred * lax.rsqrt(variance + 1e-05) * gain
+    return mean, lax.rsqrt(variance + 1e-05)
+
+
+def norm_into(ref, out_ref, gain_of, row):
+    length = ref.shape[1]
+    for start in range(0, length, STRIP):
+        cols = slice(start, min(start + STRIP, length))
+        mean, scale = norm_parts(ref, cols)
+        out_ref[:, cols] = ((ref[:, cols] - mean) * scale * gain_of(row, cols.stop - start)).astype(bf16)
 
 
 def score_slate(emb, weights, gain_of, scratch, exact):
     w_in, w_qkv, w_out, w_up, w_down = weights
-    resid_ref, query_ref, keys_ref, value_ref, mixed_ref = scratch
+    resid_ref, query_ref, keys_ref, value_ref, mixed_ref, normed_ref, inner_ref = scratch
     model, length = w_in.shape[0], emb.shape[0]
     head_dim = model // HEADS
     pack = 128 // head_dim
-    resid = lax.dot_general(w_in[...], emb, (((1,), (1,)), ((), ())), preferred_element_type=f32)
-    resid_ref[...] = resid
-    normed = norm_cols(resid, gain_of(0)).astype(bf16)
-    keys_ref[...] = jnp.dot(w_qkv[model : 2 * model], normed, preferred_element_type=f32).astype(bf16).T
-    query = jnp.dot(w_qkv[:model], normed, preferred_element_type=f32)
+    resid_ref[...] = lax.dot_general(w_in[...], emb, (((1,), (1,)), ((), ())), preferred_element_type=f32)
+    norm_into(resid_ref, normed_ref, gain_of, 0)
+    keys = jnp.dot(w_qkv[model : 2 * model], normed_ref[...], preferred_element_type=f32)
+    keys_ref[...] = keys.astype(bf16).T
+    query = jnp.dot(w_qkv[:model], normed_ref[...], preferred_element_type=f32)
     query_ref[...] = (query * (LOG2E * head_dim ** (-0.5))).astype(bf16)
-    value_ref[...] = jnp.dot(w_qkv[2 * model :], normed, preferred_element_type=f32).astype(bf16)
+    value_ref[...] = jnp.dot(w_qkv[2 * model :], normed_ref[...], preferred_element_type=f32).astype(bf16)
     zeros = jnp.zeros((head_dim, length), bf16)
     ones = jnp.ones((16, length), bf16)
 
@@ -80,26 +91,36 @@
         low = total if low is None else jnp.minimum(low, total)
         high = total if high is None else jnp.maximum(high, total)
         mixed_ref[rows, :] = (both[:head_dim] * (1.0 / total)).astype(bf16)
-    resid = resid_ref[...] + jnp.dot(w_out[...], mixed_ref[...], preferred_element_type=f32)
-    resid_ref[...] = resid
-    normed = norm_cols(resid, gain_of(1)).astype(bf16)
-    inner = jnp.dot(w_up[...], normed, preferred_element_type=f32)
-    half = 0.5 * inner
-    inner = half + half * jnp.tanh(inner * (0.7978845608028654 + 0.035677408136300125 * (inner * inner)))
-    resid = resid_ref[...] + jnp.dot(w_down[...], inner.astype(bf16), preferred_element_type=f32)
-    logits = jnp.sum(norm_cols(resid, gain_of(2)) * gain_of(3), axis=0, keepdims=True)
+    resid_ref[...] = resid_ref[...] + jnp.dot(w_out[...], mixed_ref[...], preferred_element_type=f32)
+    norm_into(resid_ref, normed_ref, gain_of, 1)
+    part = w_up.shape[0] // PARTS
+    for start in range(0, part * PARTS, part):
+        inner = jnp.dot(w_up[start : start + part], normed_ref[...], preferred_element_type=f32)
+        half = 0.5 * inner
+        inner = half + half * jnp.tanh(inner * (0.7978845608028654 + 0.035677408136300125 * (inner * inner)))
+        inner_ref[start : start + part] = inner.astype(bf16)
+    resid_ref[...] = resid_ref[...] + jnp.dot(w_down[...], inner_ref[...], preferred_element_type=f32)
+    pieces = []
+    for start in range(0, length, 128):
+        cols = slice(start, start + 128)
+        mean, scale = norm_parts(resid_ref, cols)
+        terms = (resid_ref[:, cols] - mean) * (gain_of(2, 128) * gain_of(3, 128))
+        pieces.append(jnp.sum(terms, axis=0, keepdims=True) * scale)
+    logits = jnp.concatenate(pieces, axis=1)
     shifted = logits - jnp.max(logits, axis=-1, keepdims=True)
     result = shifted - jnp.log(jnp.sum(jnp.exp(shifted), axis=-1, keepdims=True))
     return result, low, high
 
 
-def score_scratch(model, length):
+def score_scratch(model, length, inner):
     return [
         pltpu.VMEM((model, length), f32),
         pltpu.VMEM((model, length), bf16),
         pltpu.VMEM((length, model), bf16),
         pltpu.VMEM((model, length), bf16),
         pltpu.VMEM((model, length), bf16),
+        pltpu.VMEM((model, length), bf16),
+        pltpu.VMEM((inner, length), bf16),
     ]
 
 
@@ -115,7 +136,7 @@
 def spread_gains(gain_refs, target, base):
     norm_ref, final_ref, score_ref = gain_refs
     model = norm_ref.shape[1]
-    gains = [norm_ref[...], final_ref[...], score_ref[...].astype(f32), jnp.zeros((4, model), f32)]
+    gains = [norm_ref[...], final_ref[...], score_ref[...].astype(f32)[None, :], jnp.zeros((4, model), f32)]
     columns = jnp.concatenate(gains, axis=0).T
     for row in range(4):
         target[base + row * model : base + (row + 1) * model, :] = jnp.broadcast_to(
@@ -129,13 +150,13 @@
 
 
 def route(owner_ref, row_ref, asks_ref, place_ref, capacity, shards, rows, bounds):
-    slates, length = owner_ref.shape
+    slates, unused, length = owner_ref.shape
     ends = chunk_ends(capacity)
     shard = lax.broadcasted_iota(i32, (shards, length), 0)
     slots = lax.broadcasted_iota(i32, (capacity, length), 0)
     upper = lax.broadcasted_iota(i32, (length, length), 0) <= lax.broadcasted_iota(i32, (length, length), 1)
     upper = upper.astype(f32).astype(bf16)
-    hits = [(owner_ref[b : b + 1, :] == shard).astype(f32) for b in range(slates)]
+    hits = [(owner_ref[b] == shard).astype(f32) for b in range(slates)]
     within = jnp.dot(jnp.concatenate(hits, axis=0).astype(bf16), upper, preferred_element_type=f32)
     before = jnp.zeros((shards, 1), f32)
     found, late = None, None
@@ -143,12 +164,12 @@
         counts = within[b * shards : (b + 1) * shards]
         slot = jnp.sum(hits[b] * (counts + before), axis=0, keepdims=True).astype(i32) - 1
         before = before + counts[:, length - 1 : length]
-        owner, index = owner_ref[b : b + 1, :], row_ref[b : b + 1, :]
+        owner, index = owner_ref[b], row_ref[b : b + 1, :]
         place = owner * ends[0] + slot
         for start, end in zip(ends[:-1], ends[1:]):
             here = shards * start + owner * (end - start) + (slot - start)
             place = jnp.where(slot >= start, here, place)
-        place_ref[b : b + 1, :] = jnp.clip(place, 0, shards * capacity - 1)
+        place_ref[b] = jnp.clip(place, 0, shards * capacity - 1)
         over = (slot >= bounds[b]).astype(i32)
         late = over if late is None else jnp.maximum(late, over)
         at_slot = (slot == slots).astype(f32).astype(bf16)
@@ -173,7 +194,7 @@
     send_refs, refs = refs[9 : 9 + chunks], refs[9 + chunks :]
     recv_refs, refs = refs[:chunks], refs[chunks:]
     raw, turned, refs = refs[:5], refs[5:10], refs[10:]
-    scratch, refs = refs[:5], refs[5:]
+    scratch, refs = refs[:7], refs[7:]
     (
         stream_sems, raw_sems, ask_send_sem, ask_recv_sem, smem_sems,
         send_sems, recv_sems, keep_sems,
@@ -181,7 +202,7 @@
     inner = lax.axis_size("gy")
     count = lax.axis_size("gx") * inner
     here = lax.axis_index("gx") * inner + lax.axis_index("gy")
-    slates, length = owner_ref.shape
+    slates, unused, length = owner_ref.shape
     model = norm_ref.shape[1]
     ends = chunk_ends(capacity)
     starts = [0] + ends[:-1]
@@ -281,12 +302,15 @@
             stage_ref[row : row + 1, :] = rows_ref[pl.ds(index, 1), :]
         send_refs[chunk][peer] = stage_ref[:depth, :].astype(bf16)
 
+    first = [next(s for s in range(slates) if ready[s] >= chunk) for chunk in range(chunks)]
+    later = [chunk for chunk in range(AHEAD, chunks) if first[chunk] > chunk - AHEAD]
     for chunk in range(chunks):
 
         @pl.loop(1, count)
         def _(step):
             pick(chunk, step)
-            give(chunk, step).start()
+            if chunk not in later:
+                give(chunk, step).start()
 
         pick(chunk, 0)
 
@@ -315,19 +339,26 @@
     @pl.loop(0, slates)
     def _(slate):
         for chunk in range(chunks):
-            first = next(s for s in range(slates) if ready[s] >= chunk)
-
-            @pl.when(slate == first)
+
+            @pl.when(slate == first[chunk])
             def _():
                 take(chunk)
+
+        for chunk in later:
+
+            @pl.when(slate == chunk - AHEAD)
+            def _():
+                @pl.loop(1, count)
+                def _(step):
+                    give(chunk, step).start()
 
         @pl.loop(0, length // PICK)
         def _(block):
             for row in range(PICK):
                 index = block * PICK + row
-                emb_ref[pl.ds(index, 1), :] = rows_ref[pl.ds(place_smem[slate, index], 1), :]
-
-        gain_of = lambda row: widen(rows_ref, gains_base, row, model, length)
+                emb_ref[pl.ds(index, 1), :] = rows_ref[pl.ds(place_smem[slate, 0, index], 1), :]
+
+        gain_of = lambda row, cols: widen(rows_ref, gains_base, row, model, cols)
         result, low, high = score_slate(emb_ref[...].astype(bf16), turned, gain_of, scratch, False)
         out_ref[slate] = result
         bad = jnp.where((low > 1.0 / LIMIT) & (high < LIMIT), 0, 1)
@@ -341,7 +372,7 @@
 
 
 def rank(owner, row_index, gains, table, weights, capacity, shards):
-    slates, length = owner.shape
+    slates, unused, length = owner.shape
     rows, width = table.shape
     model = gains[0].shape[1]
     ends = chunk_ends(capacity)
@@ -356,7 +387,7 @@
         out_shape=[
             jax.ShapeDtypeStruct((slates, 1, length), f32),
             jax.ShapeDtypeStruct((1, 128), i32),
-            jax.ShapeDtypeStruct((slates, length), i32),
+            jax.ShapeDtypeStruct((slates, 1, length), i32),
             *[jax.ShapeDtypeStruct(block, bf16) for block in blocks],
         ],
         in_specs=[vmem, vmem, *[vmem] * 3, hbm, *[hbm] * 5],
@@ -367,7 +398,7 @@
             pltpu.VMEM((shards, 1, capacity), i32),
             pltpu.VMEM((shards, 1, capacity), i32),
             pltpu.SMEM((shards, 1, capacity), i32),
-            pltpu.SMEM((slates, length), i32),
+            pltpu.SMEM((slates, 1, length), i32),
             pltpu.VMEM((max(depths), width), f32),
             pltpu.VMEM((length, width), f32),
             pltpu.VMEM((1, length), i32),
@@ -375,7 +406,7 @@
             *[pltpu.VMEM(block, bf16) for block in blocks],
             *[pltpu.VMEM(w.shape, bf16) for w in weights],
             *[pltpu.VMEM(w.shape[::-1], bf16) for w in weights],
-            *score_scratch(model, length),
+            *score_scratch(model, length, weights[3].shape[1]),
             pltpu.SemaphoreType.DMA((BUFFERS,)),
             pltpu.SemaphoreType.DMA((5,)),
             pltpu.SemaphoreType.DMA,
@@ -394,10 +425,10 @@
 
 def finish_kernel(flag_ref, ranked_ref, place_hbm, norm_hbm, final_hbm, score_hbm, *refs):
     raw_hbm, refs = refs[:5], refs[5:]
-    chunks = len(refs) - 24
+    chunks = len(refs) - 26
     kept_refs, out_ref, refs = refs[:chunks], refs[chunks], refs[chunks + 1 :]
     rows_ref, landed_ref, emb_ref, place_ref = refs[:4]
-    gain_refs, raw, turned, scratch, sem = refs[4:7], refs[7:12], refs[12:17], refs[17:22], refs[22]
+    gain_refs, raw, turned, scratch, sem = refs[4:7], refs[7:12], refs[12:17], refs[17:24], refs[24]
     slates, length = out_ref.shape
     model = norm_hbm.shape[1]
     redo = flag_ref[0, 0] > 0
@@ -430,7 +461,7 @@
 
             base += shards * depth
         spread_gains(gain_refs, rows_ref, base)
-        gain_of = lambda row: widen(rows_ref, base, row, model, length)
+        gain_of = lambda row, cols: widen(rows_ref, base, row, model, cols)
 
         @pl.loop(0, slates)
         def _(slate):
@@ -438,7 +469,7 @@
             def _(block):
                 for row in range(PICK):
                     index = block * PICK + row
-                    emb_ref[pl.ds(index, 1), :] = rows_ref[pl.ds(place_ref[slate, index], 1), :]
+                    emb_ref[pl.ds(index, 1), :] = rows_ref[pl.ds(place_ref[slate, 0, index], 1), :]
 
             result, low, high = score_slate(emb_ref[...].astype(bf16), turned, gain_of, scratch, True)
             out_ref[pl.ds(slate, 1), :] = result
@@ -460,11 +491,11 @@
             pltpu.VMEM((shards * capacity + 4 * model, width), f32),
             pltpu.VMEM((shards, deepest, width), bf16),
             pltpu.VMEM((length, width), f32),
-            pltpu.SMEM((slates, length), i32),
+            pltpu.SMEM((slates, 1, length), i32),
             *[pltpu.VMEM(gain.shape, gain.dtype) for gain in gains],
             *[pltpu.VMEM(w.shape, bf16) for w in weights],
             *[pltpu.VMEM(w.shape[::-1], bf16) for w in weights],
-            *score_scratch(model, length),
+            *score_scratch(model, length, weights[3].shape[1]),
             pltpu.SemaphoreType.DMA,
         ],
         compiler_params=pltpu.CompilerParams(vmem_limit_bytes=60 * 1024 * 1024),
@@ -488,8 +519,8 @@
     slates, length, unused = candidate_owner.shape
     shards = lax.axis_size(("gx", "gy"))
     capacity = max(16, 2 * slates * length // shards)
-    owner = candidate_owner.reshape(slates, length)
-    gains = (norm_gains[0], final_gain[None, :], w_score[None, :])
+    owner = candidate_owner.reshape(slates, 1, length)
+    gains = (norm_gains[0], final_gain[None, :], w_score)
     weights = (w_in, w_qkv[0], w_out[0], w_up[0], w_down[0])
     ranked, flag, place, *kept = rank(owner, candidate_row, gains, item_table, weights, capacity, shards)
     return finish(flag, place, ranked, gains, weights, kept)

time: 108 us -> 95.3 us (0.88)
  Pallas kernels: 105 us -> 94.9 us
  local copies, waits for them, and re-layouts: 2.59 us -> 0 us
    pallas_call x1, Pallas kernels: 103 us -> 93.3 us  [rank(): pl.pallas_call(functools.partial(rank_kernel, capacity), out_shape=[jax.S...]
    unnamed x1 -> x0, local copies, waits for them, and re-layouts: 1.32 us -> none
    broadcast_in_dim x1 -> x0, local copies, waits for them, and re-layouts: 1.27 us -> none  [per_device(): gains = (norm_gains[0], final_gain[None, :], w_score[None, :])]
where the time goes in v2:
time: 95.3 us; the launch traced here: 95.1 us
  Pallas kernels  94.9 us (100%)
    pallas_call x1, Pallas kernels, rank(): pl.pallas_call(functools.partial(rank_kernel, capacity), out_shape=[jax.S...  93.3 us

profile of v2, /device:TPU:0, one launch (start us, length us, event | category | flops | bytes accessed | tf_op | source)
XLA Modules:
  0.0 95.1 jit_solution(12407508198557538576)
XLA Ops:
  0.0 93.3 %rank.1 = (f32[8,1,512]{2,1,0:T(1,128)}, s32[1,128]{1,0:T(1,128)}, s32[8,1,512]{2,1,0:T(1,128)}, bf16[32,64,128]{2,1,0:T(8,128)(2,1)}, bf16[32,64,128]{2,1,0:T(8...) custom-call(s32[8,1,512]{2,1,0:T(1,128)} %bitcast.15, ...), custom_call_target="tpu_custom_call" | custom-call | tf_op jit(solution)/shard_map/rank/pallas_call | solution.py:385
  93.4 1.5 %finish.1 = f32[8,512]{1,0:T(8,128)} custom-call(s32[1,128]{1,0:T(1,128)} %get-tuple-element.14.flag_ref, f32[8,1,512]{2,1,0:T(1,128)} %get-tuple-element.15.ranked_ref, s32[8,1,512]{2,1,0:T(1,128)} %get-tuple-element.16.place_hbm, f32[2,512]{1,0:T(2,128)} %bitcast.17, f32[1,512]{1,0:T(1,128)} %bitcast.19, bf16[512]{0:T(512)(128)(2,1)} %score_hbm.1, ...), custom_call_target="tpu_custom_call" | custom-call | tf_op jit(solution)/shard_map/finish/pallas_call | solution.py:485

commit v3 on v2

--- a/solution.py
+++ b/solution.py
@@ -21,7 +21,7 @@
 
 
 def chunk_ends(capacity):
-    return sorted({-(-capacity * part // 128) * 16 for part in (2, 4, 5, 6, 7, 8)})
+    return sorted({-(-capacity * part // 128) * 16 for part in (2, 3, 4, 5, 6, 7, 8)})
 
 
 def ready_chunks(capacity, slates):
@@ -354,12 +354,14 @@
 
         @pl.loop(0, length // PICK)
         def _(block):
+            start = pl.multiple_of(block * PICK, PICK)
             for row in range(PICK):
-                index = block * PICK + row
-                emb_ref[pl.ds(index, 1), :] = rows_ref[pl.ds(place_smem[slate, 0, index], 1), :]
+                index = place_smem[slate, 0, start + row]
+                stage_ref[row : row + 1, :] = rows_ref[pl.ds(index, 1), :]
+            emb_ref[pl.ds(start, PICK), :] = stage_ref[:PICK, :].astype(bf16)
 
         gain_of = lambda row, cols: widen(rows_ref, gains_base, row, model, cols)
-        result, low, high = score_slate(emb_ref[...].astype(bf16), turned, gain_of, scratch, False)
+        result, low, high = score_slate(emb_ref[...], turned, gain_of, scratch, False)
         out_ref[slate] = result
         bad = jnp.where((low > 1.0 / LIMIT) & (high < LIMIT), 0, 1)
         worst_ref[...] = jnp.maximum(jnp.where(slate == 0, late, worst_ref[...]), bad)
@@ -399,8 +401,8 @@
             pltpu.VMEM((shards, 1, capacity), i32),
             pltpu.SMEM((shards, 1, capacity), i32),
             pltpu.SMEM((slates, 1, length), i32),
-            pltpu.VMEM((max(depths), width), f32),
-            pltpu.VMEM((length, width), f32),
+            pltpu.VMEM((max(PICK, *depths), width), f32),
+            pltpu.VMEM((length, width), bf16),
             pltpu.VMEM((1, length), i32),
             *[pltpu.VMEM(block, bf16) for block in blocks],
             *[pltpu.VMEM(block, bf16) for block in blocks],

time: 95.3 us -> 92.8 us (0.974)
  Pallas kernels: 94.9 us -> 92.4 us
    pallas_call x1, Pallas kernels: 93.3 us -> 90.8 us  [rank(): pl.pallas_call(functools.partial(rank_kernel, capacity), out_shape=[jax.S...]
where the time goes in v3:
time: 92.8 us; the launch traced here: 92.5 us
  Pallas kernels  92.4 us (100%)
    pallas_call x1, Pallas kernels, rank(): pl.pallas_call(functools.partial(rank_kernel, capacity), out_shape=[jax.S...  90.8 us

profile of v3, /device:TPU:0, one launch (start us, length us, event | category | flops | bytes accessed | tf_op | source)
XLA Modules:
  0.0 92.5 jit_solution(10764453188715377144)
XLA Ops:
  0.0 90.8 %rank.1 = (f32[8,1,512]{2,1,0:T(1,128)}, s32[1,128]{1,0:T(1,128)}, s32[8,1,512]{2,1,0:T(1,128)}, bf16[32,64,128]{2,1,0:T(8,128)(2,1)}, bf16[32,32,128]{2,1,0:T(8...) custom-call(s32[8,1,512]{2,1,0:T(1,128)} %bitcast.15, ...), custom_call_target="tpu_custom_call" | custom-call | tf_op jit(solution)/shard_map/rank/pallas_call | solution.py:387
  90.8 1.5 %finish.1 = f32[8,512]{1,0:T(8,128)} custom-call(s32[1,128]{1,0:T(1,128)} %get-tuple-element.15.flag_ref, f32[8,1,512]{2,1,0:T(1,128)} %get-tuple-element.16.ranked_ref, s32[8,1,512]{2,1,0:T(1,128)} %get-tuple-element.17.place_hbm, f32[2,512]{1,0:T(2,128)} %bitcast.17, f32[1,512]{1,0:T(1,128)} %bitcast.19, bf16[512]{0:T(512)(128)(2,1)} %score_hbm.1, ...), custom_call_target="tpu_custom_call" | custom-call | tf_op jit(solution)/shard_map/finish/pallas_call | solution.py:487
